TPU v7x, 32 devices: a whole 2x2x4 slice. The times are simulated.
32 devices in a mesh: member: 2 (over x), gx: 16 (over z, y, core).
Axes of the slice: x: 2, y: 2, z: 4, core: 2. Of those that a mesh axis runs over, the one named last changes fastest.
Arguments:
- spectrum: float32 [36, 32, 256, 128], P(None, None, ('member', 'gx')), parts along dimension 2, may hold values from 0 to 1
- wind: float32 [2, 256, 128], P(None, ('member', 'gx')), parts along dimension 1, may hold values from -32 to 32
- land_sea: int32 [128, 128], P('gx'), may hold values 0 or 1
- band_rows: int32 [128], replicated, may hold values from 0 to 127, each once
Outputs:
- spectrum_next: float32 [36, 32, 256, 128], P(None, None, ('member', 'gx')), parts along dimension 2
- ocean_fields: float32 [4, 128, 256], P(None, 'gx', 'member'), parts along dimension 2
There are 2 independent parts, one for each index of `member`. A program takes and returns all parts, laid end to end along the dimension named above; an argument that names none is the same for every part. Nothing has to cross between parts.
Inputs may be any that keep to these rules, and one draw needn't show every extreme that they name: band_rows names each of the 128 latitude rows exactly once.
All inputs are finite; a program needn't handle non-finite values. No bound on the sum of `land_sea` on one device may be relied on, other than what follows from the above.
Results may differ from a plain program's by a relative error of at most 0.00015.
Values sent between devices are 32-bit elements; how exact they have to be, the bound alone decides.
A program may use at most 128 MiB of HBM per device.

v0:
```python
import math
import jax
import jax.numpy as jnp
from jax import lax
from jax.sharding import PartitionSpec as P

STEPS = 3


def passed_along(value, axis, steps):
    count = lax.axis_size(axis)
    pairs = [(source, (source + steps) % count) for source in range(count)]
    return lax.ppermute(value, axis, pairs)


def wave_tables(directions, frequencies):
    angles = (jnp.arange(directions, dtype=jnp.float32) + 0.5) * (2.0 * math.pi / directions)
    levels = jnp.arange(frequencies, dtype=jnp.float32)
    shrink = jnp.power(jnp.float32(1.1), -levels)
    frequency = 0.0418 / shrink
    inverse_speed = 2.0 * math.pi * frequency / 9.81
    weight = (levels + 1.0) / frequencies
    cosine_dir = jnp.cos(angles)[:, None]
    sine_dir = jnp.sin(angles)[:, None]
    courant_x = 0.45 * shrink[None, :] * cosine_dir
    courant_y = 0.45 * shrink[None, :] * sine_dir
    factor = 3.0 / math.sqrt(directions * frequencies)
    project = jnp.stack(
        [factor * weight[None, :] * cosine_dir, factor * weight[None, :] * sine_dir]
    )
    return (courant_x, courant_y, cosine_dir, sine_dir, inverse_speed, weight * weight, project)


def upwind(center, west_cell, east_cell, courant_x, courant_y):
    along_x = courant_x[:, :, None, None]
    along_y = courant_y[:, :, None, None]
    border = jnp.zeros_like(center[..., :1])
    south_cell = jnp.concatenate([border, center[..., :-1]], axis=3)
    north_cell = jnp.concatenate([center[..., 1:], border], axis=3)
    return (
        center
        - jnp.maximum(along_x, 0.0) * (center - west_cell)
        + jnp.maximum(-along_x, 0.0) * (east_cell - center)
        - jnp.maximum(along_y, 0.0) * (center - south_cell)
        + jnp.maximum(-along_y, 0.0) * (north_cell - center)
    )


def sources(advected, wind_east, wind_north, sea_mask, tables):
    cosine_dir, sine_dir, inverse_speed, weight_two = (tables[2], tables[3], tables[4], tables[5])
    advected = advected * sea_mask
    energy = jnp.mean(advected, axis=(0, 1))
    wind_ratio = (
        wind_east * cosine_dir[:, :, None, None] + wind_north * sine_dir[:, :, None, None]
    ) * inverse_speed[None, :, None, None]
    growth = 0.05 * jnp.clip(wind_ratio - 1.0, 0.0, 4.0)
    damping = 0.3 * weight_two[None, :, None, None] * (energy / (0.5 + energy))
    return (advected * (1.0 + growth) / (1.0 + damping), growth * advected)


def coupling_fields(input_flux, current, project):
    stress = jnp.einsum("cij,ijxy->cxy", project, input_flux, precision=lax.Precision.HIGHEST)
    stokes = jnp.einsum("cij,ijxy->cxy", project, current, precision=lax.Precision.HIGHEST)
    return jnp.concatenate([stress, stokes], axis=0)


def per_device(spectrum, wind, land_sea, band_rows):
    tables = wave_tables(spectrum.shape[0], spectrum.shape[1])
    sea_mask = land_sea.astype(jnp.float32)
    current = spectrum
    quarter = spectrum.shape[0] // 4
    east_x = jnp.concatenate([tables[0][:quarter], tables[0][3 * quarter :]], axis=0)
    east_y = jnp.concatenate([tables[1][:quarter], tables[1][3 * quarter :]], axis=0)
    west_x = tables[0][quarter : 3 * quarter]
    west_y = tables[1][quarter : 3 * quarter]
    for step_index in range(STEPS):
        eastward = jnp.concatenate([current[:quarter], current[3 * quarter :]], axis=0)
        westward = current[quarter : 3 * quarter]
        from_west = passed_along(eastward[:, :, -1:], "gx", 1)
        from_east = passed_along(westward[:, :, :1], "gx", -1)
        west_cells = jnp.concatenate([from_west, eastward[:, :, :-1]], axis=2)
        east_cells = jnp.concatenate([westward[:, :, 1:], from_east], axis=2)
        moved_east = upwind(eastward, west_cells, eastward, east_x, east_y)
        moved_west = upwind(westward, westward, east_cells, west_x, west_y)
        advected = jnp.concatenate([moved_east[:quarter], moved_west, moved_east[quarter:]], axis=0)
        current, input_flux = sources(advected, wind[0], wind[1], sea_mask, tables)
    fields = coupling_fields(input_flux, current, tables[6])
    local_rows = jnp.transpose(fields[:, :, band_rows], (0, 2, 1))
    gathered = lax.all_gather(local_rows, "gx", axis=2, tiled=True)
    band_count = local_rows.shape[1] // lax.axis_size("gx")
    ocean_fields = lax.dynamic_slice_in_dim(
        gathered, lax.axis_index("gx") * band_count, band_count, 1
    )
    return (current, ocean_fields)


def solution(mesh):
    placed = (
        P(None, None, ("member", "gx"), None),
        P(None, ("member", "gx"), None),
        P("gx", None),
        P(),
    )
    return jax.shard_map(
        per_device,
        mesh=mesh,
        in_specs=placed,
        out_specs=(P(None, None, ("member", "gx"), None), P(None, "gx", "member")),
        check_vma=False,
    )
```

profile of v0, /device:TPU:0, one launch (start us, length us, event | category | flops | bytes accessed | tf_op | source)
XLA Modules:
  0.0 96.4 jit_solution(8376153678232764763)
XLA Ops:
  0.6 1.8 %fusion.60 = (f32[9,32,8,128]{3,2,1,0:T(8,128)S(1)}, f32[9,32,8,128]{3,2,1,0:T(8,128)S(1)}) fusion(f32[36,32,8,128]{3,2,1,0:T(8,128)} %param.4), kind=kLoop, calls=%fused_computation.121 | loop fusion | bytes 4718592 | tf_op jit(solution)/shard_map/slice | solution.py:77
  2.4 0.2 copy_dynamic-update-slice_fusion.1
  2.6 0.2 copy_dynamic-update-slice_fusion
  2.9 0.7 slice.228
  3.6 0.5 collective-permute-start
  4.1 0.8 copy-done
  4.9 0.2 slice.191
  5.1 5.5 %collective-permute-start.1 = (f32[18,32,1,128]{3,1,2,0:T(8,128)S(1)}, f32[18,32,1,128]{3,1,2,0:T(8,128)S(1)}, u32[]{:S(2)}, u32[]{:S(2)}) collective-permute-start(f32[18,32,1,128]{3,1,2,0:T(8,128)S(1)} %bitcast.18), channel_id=1, source_target_pairs={{0,15},{1,0},{2,1},{3,2},{4,3},{5,4},{6,5},{7,6},{8,7},{9,8},{10,9... | collective-permute-start | bytes 884744 | tf_op jit(solution)/shard_map/ppermute | solution.py:13
  10.6 3.1 %fusion.64 = (f32[18,32,8,127]{3,1,2,0:T(8,128)}, f32[18,32,8,127]{3,1,2,0:T(8,128)}) fusion(f32[18,32,8,128]{3,1,2,0:T(8,128)S(1)} %copy_dynamic-update-slice_fusion), kind=kLoop, calls=%fused_computation.125 | loop fusion | bytes 9363456 | tf_op jit(solution)/shard_map/slice | solution.py:38
  13.7 1.6 %slice.229 = f32[18,32,7,128]{3,1,2,0:T(8,128)} slice(f32[18,32,8,128]{3,1,2,0:T(8,128)S(1)} %copy_dynamic-update-slice_fusion), slice={[0:18], [0:32], [0:7], [0:128]} | slice | bytes 4128768 | tf_op jit(solution)/shard_map/slice | solution.py:81
  15.4 0.1 broadcast_multiply_fusion.1
  15.5 0.8 fusion.59
  16.3 0.2 slice.190
  16.6 1.8 %copy.58 = f32[18,32,8,127]{3,1,2,0:T(8,128)} copy(f32[18,32,8,127]{3,2,1,0:T(8,128)S(1)} %get-tuple-element.20) | data formatting | bytes 4681728
  18.5 1.9 %copy.59 = f32[18,32,8,127]{3,1,2,0:T(8,128)} copy(f32[18,32,8,127]{3,2,1,0:T(8,128)S(1)} %get-tuple-element.21) | data formatting | bytes 4681728
  20.3 1.7 %copy.56 = f32[18,32,7,128]{3,1,2,0:T(8,128)} copy(f32[18,32,7,128]{3,2,1,0:T(8,128)S(1)} %slice.190) | data formatting | bytes 4128768
  22.0 0.1 broadcast_multiply_fusion.3
  22.1 0.1 copy.41
  22.2 0.1 multiply_add_fusion
  22.4 4.0 %fusion.16 = f32[18,32,8,128]{3,1,2,0:T(8,128)S(1)} fusion(f32[18,32,8,128]{3,1,2,0:T(8,128)S(1)} %copy_dynamic-update-slice_fusion, f32[18,32,7,128]{3,1,2,0:T(8,128)} %slice.229, f32[18,32,1,128]{3,1,2,0:T(8,128)S(1)} %collective-permute-done, f32[18,32,8,127]{3,1,2,0:T(8,128)} %get-tuple-element.35, f32[18,32,8,127]{3,1,2,0:T(8,128)} %get-tuple-element.34, ...), kind=kLoop, calls=%fused_computation.43 | loop fusion | flops 7667712 | bytes 11768832 | tf_op jit(solution)/shard_map/add | solution.py:41
  26.4 0.3 fusion.63
  26.7 1.4 %slice-done = f32[18,32,8,128]{3,2,1,0:T(8,128)S(1)} async-done(((f32[36,32,8,128]{3,2,1,0:T(8,128)}), f32[18,32,8,128]{3,2,1,0:T(8,128)S(1)}, s32[]{:S(2)}) %slice-start) | async-done | bytes 2359320 | tf_op jit(solution)/shard_map/slice | solution.py:78
  28.1 0.7 copy-done.1
  28.8 1.7 %fusion.20 = f32[18,32,8,128]{3,1,2,0:T(8,128)S(1)} fusion(f32[18,32,1,128]{3,1,2,0:T(8,128)S(1)} %collective-permute-done.1, f32[18,32,7,128]{3,1,2,0:T(8,128)S(1)} %copy-done.3, f32[18,32,8,127]{3,1,2,0:T(8,128)S(1)} %copy-done.2, f32[18,32,8,127]{3,1,2,0:T(8,128)S(1)} %copy-done.1, f32[18,32,8,128]{3,2,1,0:T(8,128)S(1)} %slice-done, ...), kind=kLoop, calls=%fused_computation.48 | loop fusion | flops 7667712 | bytes 11768832 | tf_op jit(solution)/shard_map/add | solution.py:41
  30.6 0.6 fusion.7
  31.2 0.1 multiply_add_fusion.3
  31.2 1.4 %multiply_divide_fusion.2 = f32[36,32,8,128]{3,1,2,0:T(8,128)S(1)} fusion(f32[9,32,8,128]{3,1,2,0:T(8,128)S(1)} %get-tuple-element.33, f32[18,32,8,128]{3,1,2,0:T(8,128)S(1)} %fusion.20, f32[9,32,8,128]{3,1,2,0:T(8,128)S(1)} %get-tuple-element.32, f32[32,8,128]{2,0,1:T(8,128)S(1)} %multiply_add_fusion.3, f32[32]{0:T(128)S(1)} %power_multiply_fusion, ...), kind=kLoop, calls=%fused_computation.10 | loop fusion | flops 11796480 | bytes 9719936 | tf_op jit(solution)/shard_map/div | solution.py:58
  32.6 0.9 fusion.57
  33.5 0.3 fusion.58
  33.8 0.1 collective-permute-start.2
  33.9 0.2 fusion.40
  34.2 0.2 slice.250
  34.4 4.7 %collective-permute-start.3 = (f32[18,32,1,128]{3,1,2,0:T(8,128)S(1)}, f32[18,32,1,128]{3,1,2,0:T(8,128)S(1)}, u32[]{:S(2)}, u32[]{:S(2)}) collective-permute-start(f32[18,32,1,128]{3,1,2,0:T(8,128)S(1)} %slice.251), channel_id=1, source_target_pairs={{0,15},{1,0},{2,1},{3,2},{4,3},{5,4},{6,5},{7,6},{8,7},{9,8},{10,9... | collective-permute-start | bytes 884744 | tf_op jit(solution)/shard_map/ppermute | solution.py:13
  39.1 0.9 fusion.10
  39.9 2.8 %collective-permute-done.2 = f32[18,32,1,128]{3,1,2,0:T(8,128)S(1)} collective-permute-done((f32[18,32,1,128]{3,1,2,0:T(8,128)S(1)}, f32[18,32,1,128]{3,1,2,0:T(8,128)S(1)}, u32[]{:S(2)}, u32[]{:S(2)}) %collective-permute-start.2) | collective-permute-done | bytes 294944 | tf_op jit(solution)/shard_map/ppermute | solution.py:13
  42.7 1.9 %fusion.25 = f32[18,32,8,128]{3,1,2,0:T(8,128)S(1)} fusion(f32[18,32,7,128]{3,1,2,0:T(8,128)S(1)} %fusion.40, f32[18,32,1,128]{3,1,2,0:T(8,128)S(1)} %collective-permute-done.2, f32[18,32,8,127]{3,1,2,0:T(8,128)S(1)} %get-tuple-element.31, f32[18,32,8,127]{3,1,2,0:T(8,128)S(1)} %get-tuple-element.30, f32[9,32,8,128]{3,1,2,0:T(8,128)S(1)} %get-tuple-element.18, ...), kind=kLoop, calls=%fused_computation.54 | loop fusion | flops 8257536 | bytes 11768832 | tf_op jit(solution)/shard_map/add | solution.py:41
  44.7 0.2 fusion.62
  44.9 1.8 %fusion.29 = f32[18,32,8,128]{3,1,2,0:T(8,128)S(1)} fusion(f32[18,32,1,128]{3,1,2,0:T(8,128)S(1)} %collective-permute-done.3, f32[18,32,7,128]{3,1,2,0:T(8,128)S(1)} %slice.250, f32[18,32,8,127]{3,1,2,0:T(8,128)S(1)} %get-tuple-element.17, f32[18,32,8,127]{3,1,2,0:T(8,128)S(1)} %get-tuple-element.16, f32[36,32,8,128]{3,1,2,0:T(8,128)S(1)} %multiply_divide_fusion.2, ...), kind=kLoop, calls=%fused_computation.59 | loop fusion | flops 7667712 | bytes 11768832 | tf_op jit(solution)/shard_map/add | solution.py:41
  46.7 0.6 fusion.6
  47.3 0.1 multiply_add_fusion.2
  47.4 1.4 %multiply_divide_fusion.1 = f32[36,32,8,128]{3,1,2,0:T(8,128)S(1)} fusion(f32[9,32,8,128]{3,1,2,0:T(8,128)S(1)} %get-tuple-element.29, f32[18,32,8,128]{3,1,2,0:T(8,128)S(1)} %fusion.29, f32[9,32,8,128]{3,1,2,0:T(8,128)S(1)} %get-tuple-element.28, f32[32,8,128]{2,0,1:T(8,128)S(1)} %multiply_add_fusion.2, f32[32]{0:T(128)S(1)} %power_multiply_fusion, ...), kind=kLoop, calls=%fused_computation.9 | loop fusion | flops 11796480 | bytes 9719936 | tf_op jit(solution)/shard_map/div | solution.py:58
  48.8 0.9 fusion.55
  49.6 0.3 fusion.56
  50.0 0.1 collective-permute-start.4
  50.0 0.2 fusion.39
  50.3 0.2 slice.267
  50.5 4.5 %collective-permute-start.5 = (f32[18,32,1,128]{3,1,2,0:T(8,128)S(1)}, f32[18,32,1,128]{3,1,2,0:T(8,128)S(1)}, u32[]{:S(2)}, u32[]{:S(2)}) collective-permute-start(f32[18,32,1,128]{3,1,2,0:T(8,128)S(1)} %slice.268), channel_id=1, source_target_pairs={{0,15},{1,0},{2,1},{3,2},{4,3},{5,4},{6,5},{7,6},{8,7},{9,8},{10,9... | collective-permute-start | bytes 884744 | tf_op jit(solution)/shard_map/ppermute | solution.py:13
  55.0 0.9 fusion.8
  55.9 3.0 %collective-permute-done.4 = f32[18,32,1,128]{3,1,2,0:T(8,128)S(1)} collective-permute-done((f32[18,32,1,128]{3,1,2,0:T(8,128)S(1)}, f32[18,32,1,128]{3,1,2,0:T(8,128)S(1)}, u32[]{:S(2)}, u32[]{:S(2)}) %collective-permute-start.4) | collective-permute-done | bytes 294944 | tf_op jit(solution)/shard_map/ppermute | solution.py:13
  58.9 1.9 %fusion.34 = f32[18,32,8,128]{3,1,2,0:T(8,128)S(1)} fusion(f32[18,32,7,128]{3,1,2,0:T(8,128)S(1)} %fusion.39, f32[18,32,1,128]{3,1,2,0:T(8,128)S(1)} %collective-permute-done.4, f32[18,32,8,127]{3,1,2,0:T(8,128)S(1)} %get-tuple-element.27, f32[18,32,8,127]{3,1,2,0:T(8,128)S(1)} %get-tuple-element.26, f32[9,32,8,128]{3,1,2,0:T(8,128)S(1)} %get-tuple-element.14, ...), kind=kLoop, calls=%fused_computation.65 | loop fusion | flops 8257536 | bytes 11768832 | tf_op jit(solution)/shard_map/add | solution.py:41
  60.8 0.2 fusion.61
  61.0 1.8 %fusion.38 = f32[18,32,8,128]{3,1,2,0:T(8,128)S(1)} fusion(f32[18,32,1,128]{3,1,2,0:T(8,128)S(1)} %collective-permute-done.5, f32[18,32,7,128]{3,1,2,0:T(8,128)S(1)} %slice.267, f32[18,32,8,127]{3,1,2,0:T(8,128)S(1)} %get-tuple-element.13, f32[18,32,8,127]{3,1,2,0:T(8,128)S(1)} %get-tuple-element.12, f32[36,32,8,128]{3,1,2,0:T(8,128)S(1)} %multiply_divide_fusion.1, ...), kind=kLoop, calls=%fused_computation.70 | loop fusion | flops 7667712 | bytes 11768832 | tf_op jit(solution)/shard_map/add | solution.py:41
  62.8 0.6 fusion.41
  63.4 0.1 multiply_add_fusion.1
  63.5 1.8 %fusion.4 = (f32[36,32,8,128]{3,1,2,0:T(8,128)S(1)}, f32[36,32,8,128]{3,1,2,0:T(8,128)S(1)}) fusion(f32[32]{0:T(128)S(1)} %power_multiply_fusion, f32[36,8,128]{2,1,0:T(8,128)S(1)} %multiply_add_fusion, f32[8,128]{1,0:T(8,128)S(1)} %convert_element_type.3, f32[9,32,8,128]{3,1,2,0:T(8,128)S(1)} %get-tuple-element.25, f32[18,32,8,128]{3,1,2,0:T(8,128)S(1)} %fusion.38, ...), kind=kLoop, calls=%fused_computation.12 | loop fusion | flops 12976128 | bytes 14438528 | tf_op jit(solution)/shard_map/mul | solution.py:58
  65.3 6.5 %copy.39 = f32[36,32,8,128]{3,2,1,0:T(8,128)} copy(f32[36,32,8,128]{3,1,2,0:T(8,128)S(1)} %get-tuple-element.11) | data formatting | bytes 9437184
  71.8 2.4 %fusion.45 = f32[2,8,128]{2,0,1:T(2,128)S(1)} fusion(f32[2,36,32,1]{2,0,1,3:T(2,128)S(1)} %copy.41, f32[36,32,8,128]{3,1,2,0:T(8,128)S(1)} %get-tuple-element.11), kind=kOutput, calls=%fused_computation.77 | convolution fusion | flops 28311552 | bytes 4736000 | tf_op jit(solution)/shard_map/cij,ijxy->cxy/dot_general | solution.py:63
  74.2 2.4 %fusion.42 = f32[2,8,128]{2,0,1:T(2,128)S(1)} fusion(f32[2,36,32,1]{2,0,1,3:T(2,128)S(1)} %copy.41, f32[36,32,8,128]{3,1,2,0:T(8,128)S(1)} %get-tuple-element.10), kind=kOutput, calls=%fused_computation.76 | convolution fusion | flops 28311552 | bytes 4736000 | tf_op jit(solution)/shard_map/cij,ijxy->cxy/dot_general | solution.py:62
  76.6 0.2 copy.37
  76.8 0.8 gather_fusion
  77.5 0.1 copy.38
  77.6 17.9 %all_gather.3 = f32[4,128,128]{1,0,2:T(4,128)S(1)} all-gather(f32[4,128,8]{1,0,2:T(4,128)S(1)} %copy.38), channel_id=1, replica_groups=mesh['member'=2,'gx'=16] {'gx'}, dimensions={2}, use_global_device_ids=true | all-gather | bytes 278528 | tf_op jit(solution)/shard_map/all_gather | solution.py:89
  95.5 0.2 constant_dynamic-slice_fusion
  95.7 0.7 copy.40
  (41 shorter events, 0.3 us)
Async XLA Ops:
  2.4 2.4 %copy-start = (f32[36,32,8,128]{3,2,1,0:T(8,128)S(1)}, f32[36,32,8,128]{3,2,1,0:T(8,128)}, u32[]{:S(2)}) copy-start(f32[36,32,8,128]{3,2,1,0:T(8,128)} %param.4) | copy-start | bytes 14155780
  3.6 18.8 %collective-permute-start = (f32[18,32,1,128]{3,1,2,0:T(8,128)}, f32[18,32,1,128]{3,1,2,0:T(8,128)S(1)}, u32[]{:S(2)}, u32[]{:S(2)}) collective-permute-start(f32[18,32,1,128]{3,1,2,0:T(8,128)} %slice.228), channel_id=1, source_target_pairs={{0,1},{1,2},{2,3},{3,4},{4,5},{5,6},{6,7},{7,8},{8,9},{9,10},{10,1... | collective-permute-start | bytes 884744 | tf_op jit(solution)/shard_map/ppermute | solution.py:13
  5.1 21.7 %collective-permute-start.1 = (f32[18,32,1,128]{3,1,2,0:T(8,128)S(1)}, f32[18,32,1,128]{3,1,2,0:T(8,128)S(1)}, u32[]{:S(2)}, u32[]{:S(2)}) collective-permute-start(f32[18,32,1,128]{3,1,2,0:T(8,128)S(1)} %bitcast.18), channel_id=1, source_target_pairs={{0,15},{1,0},{2,1},{3,2},{4,3},{5,4},{6,5},{7,6},{8,7},{9,8},{10,9... | collective-permute-start | bytes 884744 | tf_op jit(solution)/shard_map/ppermute | solution.py:13
  20.3 1.7 %copy-start.5 = (s32[8,128]{1,0:T(8,128)S(1)}, s32[8,128]{1,0:T(8,128)}, u32[]{:S(2)}) copy-start(s32[8,128]{1,0:T(8,128)} %param.6) | copy-start | bytes 12292
  20.3 1.7 %copy-start.4 = (f32[2,8,128]{2,1,0:T(8,128)S(1)}, f32[2,8,128]{2,1,0:T(8,128)}, u32[]{:S(2)}) copy-start(f32[2,8,128]{2,1,0:T(8,128)} %param.5) | copy-start | bytes 24580
  20.3 1.9 %copy-start.6 = (s32[128]{0:T(128)S(1)}, s32[128]{0:T(128)}, u32[]{:S(2)}) copy-start(s32[128]{0:T(128)} %param.7) | copy-start | bytes 1540
  22.4 4.3 %copy-start.2 = (f32[18,32,8,127]{3,1,2,0:T(8,128)S(1)}, f32[18,32,8,127]{3,1,2,0:T(8,128)}, u32[]{:S(2)}) copy-start(f32[18,32,8,127]{3,1,2,0:T(8,128)} %copy.59) | copy-start | bytes 7022596
  22.4 4.3 %copy-start.3 = (f32[18,32,7,128]{3,1,2,0:T(8,128)S(1)}, f32[18,32,7,128]{3,1,2,0:T(8,128)}, u32[]{:S(2)}) copy-start(f32[18,32,7,128]{3,1,2,0:T(8,128)} %copy.56) | copy-start | bytes 6193156
  26.4 1.7 %slice-start = ((f32[36,32,8,128]{3,2,1,0:T(8,128)}), f32[18,32,8,128]{3,2,1,0:T(8,128)S(1)}, s32[]{:S(2)}) async-start(f32[36,32,8,128]{3,2,1,0:T(8,128)} %param.4), calls=%async_computation | async-start | bytes 4718592 | tf_op jit(solution)/shard_map/slice | solution.py:78
  26.4 2.4 %copy-start.1 = (f32[18,32,8,127]{3,1,2,0:T(8,128)S(1)}, f32[18,32,8,127]{3,1,2,0:T(8,128)}, u32[]{:S(2)}) copy-start(f32[18,32,8,127]{3,1,2,0:T(8,128)} %copy.58) | copy-start | bytes 7022596
  33.8 8.9 %collective-permute-start.2 = (f32[18,32,1,128]{3,1,2,0:T(8,128)S(1)}, f32[18,32,1,128]{3,1,2,0:T(8,128)S(1)}, u32[]{:S(2)}, u32[]{:S(2)}) collective-permute-start(f32[18,32,1,128]{3,1,2,0:T(8,128)S(1)} %fusion.49), channel_id=1, source_target_pairs={{0,1},{1,2},{2,3},{3,4},{4,5},{5,6},{6,7},{7,8},{8,9},{9,10},{10,1... | collective-permute-start | bytes 884744 | tf_op jit(solution)/shard_map/ppermute | solution.py:13
  34.4 10.5 %collective-permute-start.3 = (f32[18,32,1,128]{3,1,2,0:T(8,128)S(1)}, f32[18,32,1,128]{3,1,2,0:T(8,128)S(1)}, u32[]{:S(2)}, u32[]{:S(2)}) collective-permute-start(f32[18,32,1,128]{3,1,2,0:T(8,128)S(1)} %slice.251), channel_id=1, source_target_pairs={{0,15},{1,0},{2,1},{3,2},{4,3},{5,4},{6,5},{7,6},{8,7},{9,8},{10,9... | collective-permute-start | bytes 884744 | tf_op jit(solution)/shard_map/ppermute | solution.py:13
  50.0 8.9 %collective-permute-start.4 = (f32[18,32,1,128]{3,1,2,0:T(8,128)S(1)}, f32[18,32,1,128]{3,1,2,0:T(8,128)S(1)}, u32[]{:S(2)}, u32[]{:S(2)}) collective-permute-start(f32[18,32,1,128]{3,1,2,0:T(8,128)S(1)} %fusion.48), channel_id=1, source_target_pairs={{0,1},{1,2},{2,3},{3,4},{4,5},{5,6},{6,7},{7,8},{8,9},{9,10},{10,1... | collective-permute-start | bytes 884744 | tf_op jit(solution)/shard_map/ppermute | solution.py:13
  50.5 10.5 %collective-permute-start.5 = (f32[18,32,1,128]{3,1,2,0:T(8,128)S(1)}, f32[18,32,1,128]{3,1,2,0:T(8,128)S(1)}, u32[]{:S(2)}, u32[]{:S(2)}) collective-permute-start(f32[18,32,1,128]{3,1,2,0:T(8,128)S(1)} %slice.268), channel_id=1, source_target_pairs={{0,15},{1,0},{2,1},{3,2},{4,3},{5,4},{6,5},{7,6},{8,7},{9,8},{10,9... | collective-permute-start | bytes 884744 | tf_op jit(solution)/shard_map/ppermute | solution.py:13
where the time goes:
time: 96.6 us; the launch traced here: 96.4 us
  local copies, waits for them, and re-layouts  29.2 us (30%)
  other arithmetic  22.3 us (23%)
  blocking collectives  17.9 us (19%)
  starting transfers between devices  15.3 us (16%)
  waiting for transfers between devices  5.77 us (6%)
  matrix products  4.79 us (5%)
  between operations  1.14 us (1%)
    all_gather x1, blocking collectives, per_device(): gathered = lax.all_gather(local_rows, 'gx', axis=2, tiled=True)  17.9 us
    ppermute x6, starting transfers between devices, passed_along(): return lax.ppermute(value, axis, pairs)  15.3 us
    unnamed x20, local copies, waits for them, and re-layouts  14.3 us
    add x6, other arithmetic, upwind(): center - jnp.maximum(along_x, 0.0) * (center - west_cell)  13.1 us
    ppermute x6, waiting for transfers between devices, passed_along(): return lax.ppermute(value, axis, pairs)  5.77 us
    slice x4, local copies, waits for them, and re-layouts, upwind(): south_cell = jnp.concatenate([border, center[..., :-1]], axis=3)  5.63 us
    div x2, other arithmetic, sources(): return (advected * (1.0 + growth) / (1.0 + damping), growth * advected)  2.77 us
    dot_general x1, matrix products, coupling_fields(): jnp.einsum('cij,ijxy->cxy', project, input_flux, precision=lax.Precision....  2.41 us
  transfers between devices with their start and end apart: 6, of which 2 were waited for; matrix products, arithmetic and copies ran while one was open for 24% of the time, Pallas kernels for 0%

commit v1 on v0

--- a/solution.py
+++ b/solution.py
@@ -3,6 +3,7 @@
 import jax.numpy as jnp
 from jax import lax
 from jax.sharding import PartitionSpec as P
+from jax.lax import all_to_all, axis_size
 
 STEPS = 3
 
@@ -86,7 +87,8 @@
         current, input_flux = sources(advected, wind[0], wind[1], sea_mask, tables)
     fields = coupling_fields(input_flux, current, tables[6])
     local_rows = jnp.transpose(fields[:, :, band_rows], (0, 2, 1))
-    gathered = lax.all_gather(local_rows, "gx", axis=2, tiled=True)
+    high = all_to_all(jnp.stack([local_rows] * axis_size("gx")), "gx", 0, 0)
+    gathered = jnp.concatenate(high, axis=2)
     band_count = local_rows.shape[1] // lax.axis_size("gx")
     ocean_fields = lax.dynamic_slice_in_dim(
         gathered, lax.axis_index("gx") * band_count, band_count, 1

time: 96.6 us -> 87.3 us (0.904)
  blocking collectives: 17.9 us -> 0 us
  starting transfers between devices: 15.3 us -> 19.9 us
  local copies, waits for them, and re-layouts: 29.2 us -> 32.3 us
    all_gather x1 -> x0, blocking collectives: 17.9 us -> none  [per_device(): gathered = lax.all_gather(local_rows, 'gx', axis=2, tiled=True)]
    all_to_all x0 -> x1, starting transfers between devices: none -> 4.44 us  [per_device(): high = all_to_all(jnp.stack([local_rows] * axis_size('gx')), 'gx', 0, 0)]
    unnamed x20 -> x22, local copies, waits for them, and re-layouts: 14.3 us -> 16.6 us
    all_to_all x0 -> x1, waiting for transfers between devices: none -> 1.15 us  [per_device(): high = all_to_all(jnp.stack([local_rows] * axis_size('gx')), 'gx', 0, 0)]
  transfers between devices with their start and end apart: 6 -> 7, of which waited for: 2 -> 3; matrix products, arithmetic and copies ran while one was open for 24% -> 37% of each run, Pallas kernels for 0% -> 0%
where the time goes in v1:
time: 87.3 us; the launch traced here: 87 us
  local copies, waits for them, and re-layouts  32.3 us (37%)
  other arithmetic  22.1 us (25%)
  starting transfers between devices  19.9 us (23%)
  waiting for transfers between devices  6.7 us (8%)
  matrix products  4.8 us (5%)
  between operations  1.16 us (1%)
    unnamed x22, local copies, waits for them, and re-layouts  16.6 us
    ppermute x6, starting transfers between devices, passed_along(): return lax.ppermute(value, axis, pairs)  15.5 us
    add x6, other arithmetic, upwind(): center - jnp.maximum(along_x, 0.0) * (center - west_cell)  13.1 us
    slice x4, local copies, waits for them, and re-layouts, upwind(): south_cell = jnp.concatenate([border, center[..., :-1]], axis=3)  5.63 us
    ppermute x6, waiting for transfers between devices, passed_along(): return lax.ppermute(value, axis, pairs)  5.55 us
    all_to_all x1, starting transfers between devices, per_device(): high = all_to_all(jnp.stack([local_rows] * axis_size('gx')), 'gx', 0, 0)  4.44 us
    div x2, other arithmetic, sources(): return (advected * (1.0 + growth) / (1.0 + damping), growth * advected)  2.77 us
    dot_general x1, matrix products, coupling_fields(): jnp.einsum('cij,ijxy->cxy', project, input_flux, precision=lax.Precision....  2.4 us
  transfers between devices with their start and end apart: 7, of which 3 were waited for; matrix products, arithmetic and copies ran while one was open for 37% of the time, Pallas kernels for 0%

profile of v1, /device:TPU:0, one launch (start us, length us, event | category | flops | bytes accessed | tf_op | source)
XLA Modules:
  0.0 87.0 jit_solution(1249808869936672601)
XLA Ops:
  0.6 1.8 %fusion.60 = (f32[9,32,8,128]{3,2,1,0:T(8,128)S(1)}, f32[9,32,8,128]{3,2,1,0:T(8,128)S(1)}) fusion(f32[36,32,8,128]{3,2,1,0:T(8,128)} %param.4), kind=kLoop, calls=%fused_computation.122 | loop fusion | bytes 4718592 | tf_op jit(solution)/shard_map/slice | solution.py:78
  2.4 0.2 copy_dynamic-update-slice_fusion.1
  2.6 0.2 copy_dynamic-update-slice_fusion
  2.9 0.7 slice.228
  3.6 0.5 collective-permute-start
  4.1 0.8 copy-done.1
  4.9 0.2 slice.191
  5.1 5.5 %collective-permute-start.1 = (f32[18,32,1,128]{3,1,2,0:T(8,128)S(1)}, f32[18,32,1,128]{3,1,2,0:T(8,128)S(1)}, u32[]{:S(2)}, u32[]{:S(2)}) collective-permute-start(f32[18,32,1,128]{3,1,2,0:T(8,128)S(1)} %bitcast.24), channel_id=1, source_target_pairs={{0,15},{1,0},{2,1},{3,2},{4,3},{5,4},{6,5},{7,6},{8,7},{9,8},{10,9... | collective-permute-start | bytes 884744 | tf_op jit(solution)/shard_map/ppermute | solution.py:14
  10.6 3.1 %fusion.64 = (f32[18,32,8,127]{3,1,2,0:T(8,128)}, f32[18,32,8,127]{3,1,2,0:T(8,128)}) fusion(f32[18,32,8,128]{3,1,2,0:T(8,128)S(1)} %copy_dynamic-update-slice_fusion), kind=kLoop, calls=%fused_computation.126 | loop fusion | bytes 9363456 | tf_op jit(solution)/shard_map/slice | solution.py:39
  13.7 1.6 %slice.229 = f32[18,32,7,128]{3,1,2,0:T(8,128)} slice(f32[18,32,8,128]{3,1,2,0:T(8,128)S(1)} %copy_dynamic-update-slice_fusion), slice={[0:18], [0:32], [0:7], [0:128]} | slice | bytes 4128768 | tf_op jit(solution)/shard_map/slice | solution.py:82
  15.4 0.1 broadcast_multiply_fusion.1
  15.5 0.8 fusion.59
  16.3 0.2 slice.190
  16.6 1.8 %copy.61 = f32[18,32,8,127]{3,1,2,0:T(8,128)} copy(f32[18,32,8,127]{3,2,1,0:T(8,128)S(1)} %get-tuple-element.18) | data formatting | bytes 4681728
  18.4 1.9 %copy.62 = f32[18,32,8,127]{3,1,2,0:T(8,128)} copy(f32[18,32,8,127]{3,2,1,0:T(8,128)S(1)} %get-tuple-element.19) | data formatting | bytes 4681728
  20.3 1.7 %copy.59 = f32[18,32,7,128]{3,1,2,0:T(8,128)} copy(f32[18,32,7,128]{3,2,1,0:T(8,128)S(1)} %slice.190) | data formatting | bytes 4128768
  22.0 0.1 broadcast_multiply_fusion.3
  22.1 0.1 copy.44
  22.2 0.1 multiply_add_fusion
  22.4 4.0 %fusion.16 = f32[18,32,8,128]{3,1,2,0:T(8,128)S(1)} fusion(f32[18,32,8,128]{3,1,2,0:T(8,128)S(1)} %copy_dynamic-update-slice_fusion, f32[18,32,7,128]{3,1,2,0:T(8,128)} %slice.229, f32[18,32,1,128]{3,1,2,0:T(8,128)S(1)} %collective-permute-done, f32[18,32,8,127]{3,1,2,0:T(8,128)} %get-tuple-element.33, f32[18,32,8,127]{3,1,2,0:T(8,128)} %get-tuple-element.32, ...), kind=kLoop, calls=%fused_computation.43 | loop fusion | flops 7667712 | bytes 11768832 | tf_op jit(solution)/shard_map/add | solution.py:42
  26.4 0.3 fusion.63
  26.7 1.4 %slice-done = f32[18,32,8,128]{3,2,1,0:T(8,128)S(1)} async-done(((f32[36,32,8,128]{3,2,1,0:T(8,128)}), f32[18,32,8,128]{3,2,1,0:T(8,128)S(1)}, s32[]{:S(2)}) %slice-start) | async-done | bytes 2359320 | tf_op jit(solution)/shard_map/slice | solution.py:79
  28.1 0.7 copy-done.2
  28.8 1.7 %fusion.20 = f32[18,32,8,128]{3,1,2,0:T(8,128)S(1)} fusion(f32[18,32,1,128]{3,1,2,0:T(8,128)S(1)} %collective-permute-done.1, f32[18,32,7,128]{3,1,2,0:T(8,128)S(1)} %copy-done.4, f32[18,32,8,127]{3,1,2,0:T(8,128)S(1)} %copy-done.3, f32[18,32,8,127]{3,1,2,0:T(8,128)S(1)} %copy-done.2, f32[18,32,8,128]{3,2,1,0:T(8,128)S(1)} %slice-done, ...), kind=kLoop, calls=%fused_computation.48 | loop fusion | flops 7667712 | bytes 11768832 | tf_op jit(solution)/shard_map/add | solution.py:42
  30.5 0.6 fusion.7
  31.1 0.1 multiply_add_fusion.3
  31.2 1.4 %multiply_divide_fusion.2 = f32[36,32,8,128]{3,1,2,0:T(8,128)S(1)} fusion(f32[9,32,8,128]{3,1,2,0:T(8,128)S(1)} %get-tuple-element.31, f32[18,32,8,128]{3,1,2,0:T(8,128)S(1)} %fusion.20, f32[9,32,8,128]{3,1,2,0:T(8,128)S(1)} %get-tuple-element.30, f32[32,8,128]{2,0,1:T(8,128)S(1)} %multiply_add_fusion.3, f32[32]{0:T(128)S(1)} %power_multiply_fusion, ...), kind=kLoop, calls=%fused_computation.10 | loop fusion | flops 11796480 | bytes 9719936 | tf_op jit(solution)/shard_map/div | solution.py:59
  32.6 0.9 fusion.57
  33.5 0.3 fusion.58
  33.9 0.2 fusion.40
  34.1 0.2 slice.250
  34.4 4.7 %collective-permute-start.3 = (f32[18,32,1,128]{3,1,2,0:T(8,128)S(1)}, f32[18,32,1,128]{3,1,2,0:T(8,128)S(1)}, u32[]{:S(2)}, u32[]{:S(2)}) collective-permute-start(f32[18,32,1,128]{3,1,2,0:T(8,128)S(1)} %slice.251), channel_id=1, source_target_pairs={{0,15},{1,0},{2,1},{3,2},{4,3},{5,4},{6,5},{7,6},{8,7},{9,8},{10,9... | collective-permute-start | bytes 884744 | tf_op jit(solution)/shard_map/ppermute | solution.py:14
  39.1 0.9 fusion.10
  39.9 2.8 %collective-permute-done.2 = f32[18,32,1,128]{3,1,2,0:T(8,128)S(1)} collective-permute-done((f32[18,32,1,128]{3,1,2,0:T(8,128)S(1)}, f32[18,32,1,128]{3,1,2,0:T(8,128)S(1)}, u32[]{:S(2)}, u32[]{:S(2)}) %collective-permute-start.2) | collective-permute-done | bytes 294944 | tf_op jit(solution)/shard_map/ppermute | solution.py:14
  42.7 1.9 %fusion.25 = f32[18,32,8,128]{3,1,2,0:T(8,128)S(1)} fusion(f32[18,32,7,128]{3,1,2,0:T(8,128)S(1)} %fusion.40, f32[18,32,1,128]{3,1,2,0:T(8,128)S(1)} %collective-permute-done.2, f32[18,32,8,127]{3,1,2,0:T(8,128)S(1)} %get-tuple-element.29, f32[18,32,8,127]{3,1,2,0:T(8,128)S(1)} %get-tuple-element.28, f32[9,32,8,128]{3,1,2,0:T(8,128)S(1)} %get-tuple-element.16, ...), kind=kLoop, calls=%fused_computation.54 | loop fusion | flops 8257536 | bytes 11768832 | tf_op jit(solution)/shard_map/add | solution.py:42
  44.6 0.2 fusion.62
  44.9 1.8 %fusion.29 = f32[18,32,8,128]{3,1,2,0:T(8,128)S(1)} fusion(f32[18,32,1,128]{3,1,2,0:T(8,128)S(1)} %collective-permute-done.3, f32[18,32,7,128]{3,1,2,0:T(8,128)S(1)} %slice.250, f32[18,32,8,127]{3,1,2,0:T(8,128)S(1)} %get-tuple-element.15, f32[18,32,8,127]{3,1,2,0:T(8,128)S(1)} %get-tuple-element.14, f32[36,32,8,128]{3,1,2,0:T(8,128)S(1)} %multiply_divide_fusion.2, ...), kind=kLoop, calls=%fused_computation.59 | loop fusion | flops 7667712 | bytes 11768832 | tf_op jit(solution)/shard_map/add | solution.py:42
  46.7 0.6 fusion.6
  47.3 0.1 multiply_add_fusion.2
  47.4 1.4 %multiply_divide_fusion.1 = f32[36,32,8,128]{3,1,2,0:T(8,128)S(1)} fusion(f32[9,32,8,128]{3,1,2,0:T(8,128)S(1)} %get-tuple-element.27, f32[18,32,8,128]{3,1,2,0:T(8,128)S(1)} %fusion.29, f32[9,32,8,128]{3,1,2,0:T(8,128)S(1)} %get-tuple-element.26, f32[32,8,128]{2,0,1:T(8,128)S(1)} %multiply_add_fusion.2, f32[32]{0:T(128)S(1)} %power_multiply_fusion, ...), kind=kLoop, calls=%fused_computation.9 | loop fusion | flops 11796480 | bytes 9719936 | tf_op jit(solution)/shard_map/div | solution.py:59
  48.7 0.9 fusion.55
  49.6 0.3 fusion.56
  50.0 0.2 fusion.39
  50.3 0.2 slice.267
  50.5 4.7 %collective-permute-start.5 = (f32[18,32,1,128]{3,1,2,0:T(8,128)S(1)}, f32[18,32,1,128]{3,1,2,0:T(8,128)S(1)}, u32[]{:S(2)}, u32[]{:S(2)}) collective-permute-start(f32[18,32,1,128]{3,1,2,0:T(8,128)S(1)} %slice.268), channel_id=1, source_target_pairs={{0,15},{1,0},{2,1},{3,2},{4,3},{5,4},{6,5},{7,6},{8,7},{9,8},{10,9... | collective-permute-start | bytes 884744 | tf_op jit(solution)/shard_map/ppermute | solution.py:14
  55.2 0.9 fusion.8
  56.1 2.8 %collective-permute-done.4 = f32[18,32,1,128]{3,1,2,0:T(8,128)S(1)} collective-permute-done((f32[18,32,1,128]{3,1,2,0:T(8,128)S(1)}, f32[18,32,1,128]{3,1,2,0:T(8,128)S(1)}, u32[]{:S(2)}, u32[]{:S(2)}) %collective-permute-start.4) | collective-permute-done | bytes 294944 | tf_op jit(solution)/shard_map/ppermute | solution.py:14
  58.8 1.9 %fusion.34 = f32[18,32,8,128]{3,1,2,0:T(8,128)S(1)} fusion(f32[18,32,7,128]{3,1,2,0:T(8,128)S(1)} %fusion.39, f32[18,32,1,128]{3,1,2,0:T(8,128)S(1)} %collective-permute-done.4, f32[18,32,8,127]{3,1,2,0:T(8,128)S(1)} %get-tuple-element.25, f32[18,32,8,127]{3,1,2,0:T(8,128)S(1)} %get-tuple-element.24, f32[9,32,8,128]{3,1,2,0:T(8,128)S(1)} %get-tuple-element.12, ...), kind=kLoop, calls=%fused_computation.65 | loop fusion | flops 8257536 | bytes 11768832 | tf_op jit(solution)/shard_map/add | solution.py:42
  60.8 0.2 fusion.61
  61.0 1.8 %fusion.38 = f32[18,32,8,128]{3,1,2,0:T(8,128)S(1)} fusion(f32[18,32,1,128]{3,1,2,0:T(8,128)S(1)} %collective-permute-done.5, f32[18,32,7,128]{3,1,2,0:T(8,128)S(1)} %slice.267, f32[18,32,8,127]{3,1,2,0:T(8,128)S(1)} %get-tuple-element.11, f32[18,32,8,127]{3,1,2,0:T(8,128)S(1)} %get-tuple-element.10, f32[36,32,8,128]{3,1,2,0:T(8,128)S(1)} %multiply_divide_fusion.1, ...), kind=kLoop, calls=%fused_computation.70 | loop fusion | flops 7667712 | bytes 11768832 | tf_op jit(solution)/shard_map/add | solution.py:42
  62.8 0.6 fusion.41
  63.4 0.1 multiply_add_fusion.1
  63.5 1.6 %fusion.4 = (f32[36,32,8,128]{3,1,2,0:T(8,128)S(1)}, f32[36,32,8,128]{3,1,2,0:T(8,128)S(1)}) fusion(f32[32]{0:T(128)S(1)} %power_multiply_fusion, f32[36,8,128]{2,1,0:T(8,128)S(1)} %multiply_add_fusion, f32[8,128]{1,0:T(8,128)S(1)} %convert_element_type.3, f32[9,32,8,128]{3,1,2,0:T(8,128)S(1)} %get-tuple-element.23, f32[18,32,8,128]{3,1,2,0:T(8,128)S(1)} %fusion.38, ...), kind=kLoop, calls=%fused_computation.12 | loop fusion | flops 12976128 | bytes 14438528 | tf_op jit(solution)/shard_map/mul | solution.py:59
  65.0 2.4 %fusion.42 = f32[2,8,128]{2,0,1:T(2,128)S(1)} fusion(f32[2,36,32,1]{2,0,1,3:T(2,128)S(1)} %copy.44, f32[36,32,8,128]{3,1,2,0:T(8,128)S(1)} %get-tuple-element.8), kind=kOutput, calls=%fused_computation.76 | convolution fusion | flops 28311552 | bytes 4736000 | tf_op jit(solution)/shard_map/cij,ijxy->cxy/dot_general | solution.py:63
  67.4 2.4 %fusion.45 = f32[2,8,128]{2,0,1:T(2,128)S(1)} fusion(f32[2,36,32,1]{2,0,1,3:T(2,128)S(1)} %copy.44, f32[36,32,8,128]{3,1,2,0:T(8,128)S(1)} %get-tuple-element.9), kind=kOutput, calls=%fused_computation.77 | convolution fusion | flops 28311552 | bytes 4736000 | tf_op jit(solution)/shard_map/cij,ijxy->cxy/dot_general | solution.py:64
  69.9 0.2 copy.39
  70.0 0.8 gather_fusion
  70.8 0.1 copy.40
  70.9 0.8 stack.5
  71.6 4.4 %all-to-all-start = ((f32[16,4,128,8]{2,3,1,0:T(8,128)}), f32[16,4,128,8]{2,3,1,0:T(8,128)S(1)}, u32[]{:S(2)}, u32[]{:S(2)}) async-start(f32[16,4,128,8]{2,3,1,0:T(8,128)} %stack.5), calls=%async_computation | async-start | bytes 524288 | tf_op jit(solution)/shard_map/all_to_all | solution.py:90
  76.1 8.9 %copy.42 = f32[36,32,8,128]{3,2,1,0:T(8,128)} copy(f32[36,32,8,128]{3,1,2,0:T(8,128)} %copy-done) | data formatting | bytes 9437184
  85.0 1.1 %all-to-all-done = f32[16,4,128,8]{2,3,1,0:T(8,128)S(1)} async-done(((f32[16,4,128,8]{2,3,1,0:T(8,128)}), f32[16,4,128,8]{2,3,1,0:T(8,128)S(1)}, u32[]{:S(2)}, u32[]{:S(2)}) %all-to-all-start) | async-done | bytes 262176 | tf_op jit(solution)/shard_map/all_to_all | solution.py:90
  86.1 0.1 constant_dynamic-slice_fusion
  86.3 0.7 copy.43
  (46 shorter events, 0.5 us)
Async XLA Ops:
  2.4 2.4 %copy-start.1 = (f32[36,32,8,128]{3,2,1,0:T(8,128)S(1)}, f32[36,32,8,128]{3,2,1,0:T(8,128)}, u32[]{:S(2)}) copy-start(f32[36,32,8,128]{3,2,1,0:T(8,128)} %param.4) | copy-start | bytes 14155780
  3.6 18.8 %collective-permute-start = (f32[18,32,1,128]{3,1,2,0:T(8,128)}, f32[18,32,1,128]{3,1,2,0:T(8,128)S(1)}, u32[]{:S(2)}, u32[]{:S(2)}) collective-permute-start(f32[18,32,1,128]{3,1,2,0:T(8,128)} %slice.228), channel_id=1, source_target_pairs={{0,1},{1,2},{2,3},{3,4},{4,5},{5,6},{6,7},{7,8},{8,9},{9,10},{10,1... | collective-permute-start | bytes 884744 | tf_op jit(solution)/shard_map/ppermute | solution.py:14
  5.1 21.7 %collective-permute-start.1 = (f32[18,32,1,128]{3,1,2,0:T(8,128)S(1)}, f32[18,32,1,128]{3,1,2,0:T(8,128)S(1)}, u32[]{:S(2)}, u32[]{:S(2)}) collective-permute-start(f32[18,32,1,128]{3,1,2,0:T(8,128)S(1)} %bitcast.24), channel_id=1, source_target_pairs={{0,15},{1,0},{2,1},{3,2},{4,3},{5,4},{6,5},{7,6},{8,7},{9,8},{10,9... | collective-permute-start | bytes 884744 | tf_op jit(solution)/shard_map/ppermute | solution.py:14
  20.3 1.7 %copy-start.6 = (s32[8,128]{1,0:T(8,128)S(1)}, s32[8,128]{1,0:T(8,128)}, u32[]{:S(2)}) copy-start(s32[8,128]{1,0:T(8,128)} %param.6) | copy-start | bytes 12292
  20.3 1.7 %copy-start.5 = (f32[2,8,128]{2,1,0:T(8,128)S(1)}, f32[2,8,128]{2,1,0:T(8,128)}, u32[]{:S(2)}) copy-start(f32[2,8,128]{2,1,0:T(8,128)} %param.5) | copy-start | bytes 24580
  20.3 1.9 %copy-start.7 = (s32[128]{0:T(128)S(1)}, s32[128]{0:T(128)}, u32[]{:S(2)}) copy-start(s32[128]{0:T(128)} %param.7) | copy-start | bytes 1540
  22.4 4.3 %copy-start.3 = (f32[18,32,8,127]{3,1,2,0:T(8,128)S(1)}, f32[18,32,8,127]{3,1,2,0:T(8,128)}, u32[]{:S(2)}) copy-start(f32[18,32,8,127]{3,1,2,0:T(8,128)} %copy.62) | copy-start | bytes 7022596
  22.4 4.3 %copy-start.4 = (f32[18,32,7,128]{3,1,2,0:T(8,128)S(1)}, f32[18,32,7,128]{3,1,2,0:T(8,128)}, u32[]{:S(2)}) copy-start(f32[18,32,7,128]{3,1,2,0:T(8,128)} %copy.59) | copy-start | bytes 6193156
  26.4 1.7 %slice-start = ((f32[36,32,8,128]{3,2,1,0:T(8,128)}), f32[18,32,8,128]{3,2,1,0:T(8,128)S(1)}, s32[]{:S(2)}) async-start(f32[36,32,8,128]{3,2,1,0:T(8,128)} %param.4), calls=%async_computation.1 | async-start | bytes 4718592 | tf_op jit(solution)/shard_map/slice | solution.py:79
  26.4 2.4 %copy-start.2 = (f32[18,32,8,127]{3,1,2,0:T(8,128)S(1)}, f32[18,32,8,127]{3,1,2,0:T(8,128)}, u32[]{:S(2)}) copy-start(f32[18,32,8,127]{3,1,2,0:T(8,128)} %copy.61) | copy-start | bytes 7022596
  33.8 8.9 %collective-permute-start.2 = (f32[18,32,1,128]{3,1,2,0:T(8,128)S(1)}, f32[18,32,1,128]{3,1,2,0:T(8,128)S(1)}, u32[]{:S(2)}, u32[]{:S(2)}) collective-permute-start(f32[18,32,1,128]{3,1,2,0:T(8,128)S(1)} %fusion.49), channel_id=1, source_target_pairs={{0,1},{1,2},{2,3},{3,4},{4,5},{5,6},{6,7},{7,8},{8,9},{9,10},{10,1... | collective-permute-start | bytes 884744 | tf_op jit(solution)/shard_map/ppermute | solution.py:14
  34.4 10.5 %collective-permute-start.3 = (f32[18,32,1,128]{3,1,2,0:T(8,128)S(1)}, f32[18,32,1,128]{3,1,2,0:T(8,128)S(1)}, u32[]{:S(2)}, u32[]{:S(2)}) collective-permute-start(f32[18,32,1,128]{3,1,2,0:T(8,128)S(1)} %slice.251), channel_id=1, source_target_pairs={{0,15},{1,0},{2,1},{3,2},{4,3},{5,4},{6,5},{7,6},{8,7},{9,8},{10,9... | collective-permute-start | bytes 884744 | tf_op jit(solution)/shard_map/ppermute | solution.py:14
  49.9 8.9 %collective-permute-start.4 = (f32[18,32,1,128]{3,1,2,0:T(8,128)S(1)}, f32[18,32,1,128]{3,1,2,0:T(8,128)S(1)}, u32[]{:S(2)}, u32[]{:S(2)}) collective-permute-start(f32[18,32,1,128]{3,1,2,0:T(8,128)S(1)} %fusion.48), channel_id=1, source_target_pairs={{0,1},{1,2},{2,3},{3,4},{4,5},{5,6},{6,7},{7,8},{8,9},{9,10},{10,1... | collective-permute-start | bytes 884744 | tf_op jit(solution)/shard_map/ppermute | solution.py:14
  50.5 10.5 %collective-permute-start.5 = (f32[18,32,1,128]{3,1,2,0:T(8,128)S(1)}, f32[18,32,1,128]{3,1,2,0:T(8,128)S(1)}, u32[]{:S(2)}, u32[]{:S(2)}) collective-permute-start(f32[18,32,1,128]{3,1,2,0:T(8,128)S(1)} %slice.268), channel_id=1, source_target_pairs={{0,15},{1,0},{2,1},{3,2},{4,3},{5,4},{6,5},{7,6},{8,7},{9,8},{10,9... | collective-permute-start | bytes 884744 | tf_op jit(solution)/shard_map/ppermute | solution.py:14
  65.0 2.4 %copy-start = (f32[36,32,8,128]{3,1,2,0:T(8,128)}, f32[36,32,8,128]{3,1,2,0:T(8,128)S(1)}, u32[]{:S(2)}) copy-start(f32[36,32,8,128]{3,1,2,0:T(8,128)S(1)} %get-tuple-element.9) | copy-start | bytes 14155780
  71.6 14.5 %all-to-all-start = ((f32[16,4,128,8]{2,3,1,0:T(8,128)}), f32[16,4,128,8]{2,3,1,0:T(8,128)S(1)}, u32[]{:S(2)}, u32[]{:S(2)}) async-start(f32[16,4,128,8]{2,3,1,0:T(8,128)} %stack.5), calls=%async_computation | async-start | bytes 524288 | tf_op jit(solution)/shard_map/all_to_all | solution.py:90
